TPU v7x, 256 devices: a whole 4x4x8 slice. The times are simulated.
256 devices in a mesh: row: 8 (over z), col: 32 (over y, x, core).
Axes of the slice: x: 4, y: 4, z: 8, core: 2. Of those that a mesh axis runs over, the one named last changes fastest.
Arguments:
- factor: bfloat16 [131072, 5, 1024], P('col', None, 'row'), may hold values from -0.0625 to 0.0625
- diag_inverse: bfloat16 [5, 1024, 1024], P(None, 'row'), may hold values from -1 to 2
- right_side: float32 [16, 128, 1024], P(None, 'col', 'row'), may hold values from -6 to 6
- tile_order: int32 [128], replicated, may hold values from 0 to 127, each once
- live_segments: int32 [16], replicated, may hold values from 2 to 5
Outputs:
- result: float32 [16, 128, 1024], P(None, 'col', 'row')
Inputs may be any that keep to these rules, and one draw needn't show every extreme that they name: `tile_order`: each of 0 to 127 appears once.
All inputs are finite; a program needn't handle non-finite values.
Results may differ from a plain program's by a relative error of at most 0.0019.
Values may be sent and summed in bfloat16 or wider, within the bound.
A program may use at most 64 MiB of HBM per device.

v0:
```python
import jax
import jax.numpy as jnp
from jax import lax
from jax.sharding import Mesh
from jax.sharding import PartitionSpec as P

COL = ("col_0", "col_1", "col_2")


def sent_to_all(array, axis):
    peers = lax.axis_size(axis)
    return lax.all_to_all(
        jnp.broadcast_to(array[None], (peers, *array.shape)), axis, 0, 0, tiled=True
    )


def taken_together(array, axis):
    return sent_to_all(array, axis).sum(axis=0)


def spread(array, axes, root):
    array = jnp.where(lax.axis_index(axes) == root, array, jnp.zeros_like(array))
    for axis in axes:
        array = lax.psum(array, axis)
    return array


def in_blocks(array, dim, peers):
    before, after = (array.shape[:dim], array.shape[dim + 1 :])
    return jnp.moveaxis(array.reshape(*before, peers, -1, *after), dim, 0)


def summed_on_arrival(array, axis, dim):
    pieces = in_blocks(array, dim, lax.axis_size(axis))
    arrived = lax.all_to_all(pieces, axis, split_axis=0, concat_axis=0, tiled=True)
    return arrived.sum(axis=0)


def per_device(factor, diag_inverse, right_side, tile_order, live_segments):
    section_count = diag_inverse.shape[0]
    slice_width = diag_inverse.shape[1]
    tile_width = diag_inverse.shape[2]
    rhs_count = right_side.shape[0]
    rows_dev = right_side.shape[1]
    my_col = lax.axis_index(COL)
    my_row = lax.axis_index("row")
    slice_start = my_row * slice_width
    partial_value = jnp.zeros((rhs_count, rows_dev * tile_width), jnp.float32)
    result = jnp.zeros((rhs_count, rows_dev, slice_width), jnp.float32)
    for section in range(section_count):
        slot_id = tile_order[section]
        root_col = slot_id // rows_dev
        local_pos = slot_id % rows_dev
        part_tile = lax.dynamic_slice_in_dim(partial_value, local_pos * tile_width, tile_width, 1)
        rhs_slice = lax.dynamic_index_in_dim(right_side, local_pos, 1, keepdims=False)
        placed = lax.dynamic_update_slice_in_dim(
            jnp.zeros((rhs_count, tile_width), jnp.float32), rhs_slice, slice_start, 1
        )
        remaining = taken_together(placed - part_tile, "row")
        inverse = diag_inverse[section].astype(jnp.float32)
        solved = lax.dot_general(
            remaining,
            inverse,
            (((1,), (1,)), ((), ())),
            precision=lax.Precision.HIGHEST,
            preferred_element_type=jnp.float32,
        )
        is_live = (section < live_segments)[:, None]
        sent_block = jnp.where(is_live, solved, jnp.zeros_like(solved)).astype(jnp.bfloat16)
        sent_block = spread(sent_block, COL, root_col)
        kept_part = lax.dynamic_slice_in_dim(remaining, slice_start, slice_width, 1)
        stored = jnp.where(is_live, solved, kept_part)
        written = lax.dynamic_update_slice_in_dim(result, stored[:, None, :], local_pos, 1)
        result = jnp.where(my_col == root_col, written, result)
        panel_rows = factor[:, section, :]
        partial_value = partial_value + lax.dot_general(
            sent_block, panel_rows, (((1,), (1,)), ((), ())), preferred_element_type=jnp.float32
        )
    shaped = partial_value.reshape(rhs_count, rows_dev, tile_width)
    total_part = summed_on_arrival(shaped, "row", 2)
    local_slots = my_col * rows_dev + jnp.arange(rows_dev, dtype=jnp.int32)
    visited = jnp.any(local_slots[:, None] == tile_order[:section_count][None, :], axis=1)
    return jnp.where(visited[None, :, None], result, right_side - total_part)


def solution(mesh):
    finer = Mesh(
        mesh.devices.reshape(mesh.shape["row"], 4, 4, 2), ("row", "col_0", "col_1", "col_2")
    )
    return jax.shard_map(
        per_device,
        mesh=finer,
        in_specs=(P(COL, None, "row"), P(None, "row", None), P(None, COL, "row"), P(), P()),
        out_specs=P(None, COL, "row"),
        check_vma=False,
    )
```

profile of v0, /device:TPU:32, one launch (start us, length us, event | category | flops | bytes accessed | tf_op | source)
XLA Modules:
  0.0 259.2 jit_solution(9069226407396317049)
XLA Ops:
  0.0 1.5 fusion.37
  11.1 1.0 constant_dynamic-slice_fusion.2
  12.1 0.8 broadcast_in_dim.114
  12.9 8.6 %all-to-all-start = ((f32[8,16,1024]{2,1,0:T(8,128)}), f32[8,16,1024]{2,1,0:T(8,128)S(1)}, u32[]{:S(2)}, u32[]{:S(2)}) async-start(f32[8,16,1024]{2,1,0:T(8,128)} %broadcast_in_dim.114), calls=%async_computation | async-start | bytes 1048576 | tf_op jit(solution)/shard_map/all_to_all | solution.py:12
  22.2 0.7 broadcast_compare_fusion
  22.8 14.7 %all-to-all-done = f32[8,16,1024]{2,1,0:T(8,128)S(1)} async-done(((f32[8,16,1024]{2,1,0:T(8,128)}), f32[8,16,1024]{2,1,0:T(8,128)S(1)}, u32[]{:S(2)}, u32[]{:S(2)}) %all-to-all-start) | async-done | bytes 524320 | tf_op jit(solution)/shard_map/all_to_all | solution.py:12
  37.6 1.3 bitcast_dynamic-update-slice_fusion
  38.9 10.7 %psum.105 = bf16[16,128]{1,0:T(8,128)(2,1)S(1)} all-reduce(bf16[16,128]{1,0:T(8,128)(2,1)S(1)} %fusion.32), channel_id=1, replica_groups=mesh['row'=8,'col_0'=4,'col_1'=4,'col_2'=2] {'col_0'}, use_global_device_ids=true, to_apply=%region_2.3 | all-reduce | flops 2048 | bytes 8192 | tf_op jit(solution)/shard_map/psum | solution.py:24
  49.7 10.5 %psum.106 = bf16[16,128]{1,0:T(8,128)(2,1)S(1)} all-reduce(bf16[16,128]{1,0:T(8,128)(2,1)S(1)} %psum.105), channel_id=1, replica_groups=mesh['row'=8,'col_0'=4,'col_1'=4,'col_2'=2] {'col_1'}, use_global_device_ids=true, to_apply=%region_3.4 | all-reduce | flops 2048 | bytes 8192 | tf_op jit(solution)/shard_map/psum | solution.py:24
  60.2 2.5 psum.107
  62.6 1.6 fusion.5
  64.3 0.8 broadcast_in_dim.116
  65.1 4.9 %all-to-all-start.1 = ((f32[8,16,1024]{2,1,0:T(8,128)}), f32[8,16,1024]{2,1,0:T(8,128)S(1)}, u32[]{:S(2)}, u32[]{:S(2)}) async-start(f32[8,16,1024]{2,1,0:T(8,128)} %broadcast_in_dim.116), calls=%async_computation.1 | async-start | bytes 1048576 | tf_op jit(solution)/shard_map/all_to_all | solution.py:12
  70.7 16.0 %all-to-all-done.1 = f32[8,16,1024]{2,1,0:T(8,128)S(1)} async-done(((f32[8,16,1024]{2,1,0:T(8,128)}), f32[8,16,1024]{2,1,0:T(8,128)S(1)}, u32[]{:S(2)}, u32[]{:S(2)}) %all-to-all-start.1) | async-done | bytes 524320 | tf_op jit(solution)/shard_map/all_to_all | solution.py:12
  86.7 0.3 fusion.31
  87.1 7.7 %psum.108 = bf16[16,128]{1,0:T(8,128)(2,1)S(1)} all-reduce(bf16[16,128]{1,0:T(8,128)(2,1)S(1)} %fusion.33), channel_id=1, replica_groups=mesh['row'=8,'col_0'=4,'col_1'=4,'col_2'=2] {'col_0'}, use_global_device_ids=true, to_apply=%region_6.7 | all-reduce | flops 2048 | bytes 8192 | tf_op jit(solution)/shard_map/psum | solution.py:24
  94.8 7.8 %psum.109 = bf16[16,128]{1,0:T(8,128)(2,1)S(1)} all-reduce(bf16[16,128]{1,0:T(8,128)(2,1)S(1)} %psum.108), channel_id=1, replica_groups=mesh['row'=8,'col_0'=4,'col_1'=4,'col_2'=2] {'col_1'}, use_global_device_ids=true, to_apply=%region_7.8 | all-reduce | flops 2048 | bytes 8192 | tf_op jit(solution)/shard_map/psum | solution.py:24
  102.6 2.5 psum.110
  105.1 1.6 convolution_add_fusion.3
  106.7 0.8 broadcast_in_dim.119
  107.5 4.8 %all-to-all-start.2 = ((f32[8,16,1024]{2,1,0:T(8,128)}), f32[8,16,1024]{2,1,0:T(8,128)S(1)}, u32[]{:S(2)}, u32[]{:S(2)}) async-start(f32[8,16,1024]{2,1,0:T(8,128)} %broadcast_in_dim.119), calls=%async_computation.2 | async-start | bytes 1048576 | tf_op jit(solution)/shard_map/all_to_all | solution.py:12
  113.0 16.0 %all-to-all-done.2 = f32[8,16,1024]{2,1,0:T(8,128)S(1)} async-done(((f32[8,16,1024]{2,1,0:T(8,128)}), f32[8,16,1024]{2,1,0:T(8,128)S(1)}, u32[]{:S(2)}, u32[]{:S(2)}) %all-to-all-start.2) | async-done | bytes 524320 | tf_op jit(solution)/shard_map/all_to_all | solution.py:12
  129.1 0.3 fusion.30
  129.5 9.7 %psum.111 = bf16[16,128]{1,0:T(8,128)(2,1)S(1)} all-reduce(bf16[16,128]{1,0:T(8,128)(2,1)S(1)} %fusion.34), channel_id=1, replica_groups=mesh['row'=8,'col_0'=4,'col_1'=4,'col_2'=2] {'col_0'}, use_global_device_ids=true, to_apply=%region_10.11 | all-reduce | flops 2048 | bytes 8192 | tf_op jit(solution)/shard_map/psum | solution.py:24
  139.2 9.8 %psum.112 = bf16[16,128]{1,0:T(8,128)(2,1)S(1)} all-reduce(bf16[16,128]{1,0:T(8,128)(2,1)S(1)} %psum.111), channel_id=1, replica_groups=mesh['row'=8,'col_0'=4,'col_1'=4,'col_2'=2] {'col_1'}, use_global_device_ids=true, to_apply=%region_11.12 | all-reduce | flops 2048 | bytes 8192 | tf_op jit(solution)/shard_map/psum | solution.py:24
  149.0 2.5 psum.113
  151.4 1.6 convolution_add_fusion.2
  153.1 0.8 broadcast_in_dim.122
  153.9 4.8 %all-to-all-start.3 = ((f32[8,16,1024]{2,1,0:T(8,128)}), f32[8,16,1024]{2,1,0:T(8,128)S(1)}, u32[]{:S(2)}, u32[]{:S(2)}) async-start(f32[8,16,1024]{2,1,0:T(8,128)} %broadcast_in_dim.122), calls=%async_computation.3 | async-start | bytes 1048576 | tf_op jit(solution)/shard_map/all_to_all | solution.py:12
  159.5 15.9 %all-to-all-done.3 = f32[8,16,1024]{2,1,0:T(8,128)S(1)} async-done(((f32[8,16,1024]{2,1,0:T(8,128)}), f32[8,16,1024]{2,1,0:T(8,128)S(1)}, u32[]{:S(2)}, u32[]{:S(2)}) %all-to-all-start.3) | async-done | bytes 524320 | tf_op jit(solution)/shard_map/all_to_all | solution.py:12
  175.5 0.3 fusion.29
  175.9 7.7 %psum.114 = bf16[16,128]{1,0:T(8,128)(2,1)S(1)} all-reduce(bf16[16,128]{1,0:T(8,128)(2,1)S(1)} %fusion.35), channel_id=1, replica_groups=mesh['row'=8,'col_0'=4,'col_1'=4,'col_2'=2] {'col_0'}, use_global_device_ids=true, to_apply=%region_14.15 | all-reduce | flops 2048 | bytes 8192 | tf_op jit(solution)/shard_map/psum | solution.py:24
  183.6 7.8 %psum.115 = bf16[16,128]{1,0:T(8,128)(2,1)S(1)} all-reduce(bf16[16,128]{1,0:T(8,128)(2,1)S(1)} %psum.114), channel_id=1, replica_groups=mesh['row'=8,'col_0'=4,'col_1'=4,'col_2'=2] {'col_1'}, use_global_device_ids=true, to_apply=%region_15.16 | all-reduce | flops 2048 | bytes 8192 | tf_op jit(solution)/shard_map/psum | solution.py:24
  191.4 2.5 psum.116
  193.8 1.6 convolution_add_fusion.1
  195.5 0.8 broadcast_in_dim.125
  196.3 4.8 %all-to-all-start.4 = ((f32[8,16,1024]{2,1,0:T(8,128)}), f32[8,16,1024]{2,1,0:T(8,128)S(1)}, u32[]{:S(2)}, u32[]{:S(2)}) async-start(f32[8,16,1024]{2,1,0:T(8,128)} %broadcast_in_dim.125), calls=%async_computation.4 | async-start | bytes 1048576 | tf_op jit(solution)/shard_map/all_to_all | solution.py:12
  201.8 16.0 %all-to-all-done.4 = f32[8,16,1024]{2,1,0:T(8,128)S(1)} async-done(((f32[8,16,1024]{2,1,0:T(8,128)}), f32[8,16,1024]{2,1,0:T(8,128)S(1)}, u32[]{:S(2)}, u32[]{:S(2)}) %all-to-all-start.4) | async-done | bytes 524320 | tf_op jit(solution)/shard_map/all_to_all | solution.py:12
  217.9 0.3 fusion.28
  218.3 9.7 %psum.117 = bf16[16,128]{1,0:T(8,128)(2,1)S(1)} all-reduce(bf16[16,128]{1,0:T(8,128)(2,1)S(1)} %fusion.36), channel_id=1, replica_groups=mesh['row'=8,'col_0'=4,'col_1'=4,'col_2'=2] {'col_0'}, use_global_device_ids=true, to_apply=%region_18.19 | all-reduce | flops 2048 | bytes 8192 | tf_op jit(solution)/shard_map/psum | solution.py:24
  228.0 9.8 %psum.118 = bf16[16,128]{1,0:T(8,128)(2,1)S(1)} all-reduce(bf16[16,128]{1,0:T(8,128)(2,1)S(1)} %psum.117), channel_id=1, replica_groups=mesh['row'=8,'col_0'=4,'col_1'=4,'col_2'=2] {'col_1'}, use_global_device_ids=true, to_apply=%region_19.20 | all-reduce | flops 2048 | bytes 8192 | tf_op jit(solution)/shard_map/psum | solution.py:24
  237.7 2.5 psum.119
  240.2 1.6 fusion
  241.9 0.8 copy.25
  242.7 4.8 %all-to-all-start.5 = ((f32[8,16,4,128]{3,2,1,0:T(4,128)}), f32[8,16,4,128]{3,2,1,0:T(4,128)S(1)}, u32[]{:S(2)}, u32[]{:S(2)}) async-start(f32[8,16,4,128]{3,2,1,0:T(4,128)} %bitcast.84), calls=%async_computation.5 | async-start | bytes 524288 | tf_op jit(solution)/shard_map/all_to_all | solution.py:35
  247.4 0.2 compare_reduce_fusion
  247.6 10.9 %all-to-all-done.5 = f32[8,16,4,128]{3,2,1,0:T(4,128)S(1)} async-done(((f32[8,16,4,128]{3,2,1,0:T(4,128)}), f32[8,16,4,128]{3,2,1,0:T(4,128)S(1)}, u32[]{:S(2)}, u32[]{:S(2)}) %all-to-all-start.5) | async-done | bytes 262176 | tf_op jit(solution)/shard_map/all_to_all | solution.py:35
  258.6 0.6 copy.17
  (35 shorter events, 1.0 us)
Async XLA Ops:
  0.0 86.7 %copy-start = (bf16[5,128,1024]{2,1,0:T(8,128)(2,1)S(1)}, bf16[5,128,1024]{2,1,0:T(8,128)(2,1)}, u32[]{:S(2)}) copy-start(bf16[5,128,1024]{2,1,0:T(8,128)(2,1)} %param.6) | copy-start | bytes 3932164
  12.9 24.6 %all-to-all-start = ((f32[8,16,1024]{2,1,0:T(8,128)}), f32[8,16,1024]{2,1,0:T(8,128)S(1)}, u32[]{:S(2)}, u32[]{:S(2)}) async-start(f32[8,16,1024]{2,1,0:T(8,128)} %broadcast_in_dim.114), calls=%async_computation | async-start | bytes 1048576 | tf_op jit(solution)/shard_map/all_to_all | solution.py:12
  65.1 21.5 %all-to-all-start.1 = ((f32[8,16,1024]{2,1,0:T(8,128)}), f32[8,16,1024]{2,1,0:T(8,128)S(1)}, u32[]{:S(2)}, u32[]{:S(2)}) async-start(f32[8,16,1024]{2,1,0:T(8,128)} %broadcast_in_dim.116), calls=%async_computation.1 | async-start | bytes 1048576 | tf_op jit(solution)/shard_map/all_to_all | solution.py:12
  107.5 21.5 %all-to-all-start.2 = ((f32[8,16,1024]{2,1,0:T(8,128)}), f32[8,16,1024]{2,1,0:T(8,128)S(1)}, u32[]{:S(2)}, u32[]{:S(2)}) async-start(f32[8,16,1024]{2,1,0:T(8,128)} %broadcast_in_dim.119), calls=%async_computation.2 | async-start | bytes 1048576 | tf_op jit(solution)/shard_map/all_to_all | solution.py:12
  153.0 94.4 %copy-start.2 = (s32[128]{0:T(128)S(1)}, s32[128]{0:T(128)}, u32[]{:S(2)}) copy-start(s32[128]{0:T(128)} %param.8) | copy-start | bytes 1540
  153.1 105.5 %copy-start.1 = (f32[16,4,128]{2,1,0:T(4,128)S(1)}, f32[16,4,128]{2,1,0:T(4,128)}, u32[]{:S(2)}) copy-start(f32[16,4,128]{2,1,0:T(4,128)} %param.7) | copy-start | bytes 98308
  153.9 21.5 %all-to-all-start.3 = ((f32[8,16,1024]{2,1,0:T(8,128)}), f32[8,16,1024]{2,1,0:T(8,128)S(1)}, u32[]{:S(2)}, u32[]{:S(2)}) async-start(f32[8,16,1024]{2,1,0:T(8,128)} %broadcast_in_dim.122), calls=%async_computation.3 | async-start | bytes 1048576 | tf_op jit(solution)/shard_map/all_to_all | solution.py:12
  196.3 21.5 %all-to-all-start.4 = ((f32[8,16,1024]{2,1,0:T(8,128)}), f32[8,16,1024]{2,1,0:T(8,128)S(1)}, u32[]{:S(2)}, u32[]{:S(2)}) async-start(f32[8,16,1024]{2,1,0:T(8,128)} %broadcast_in_dim.125), calls=%async_computation.4 | async-start | bytes 1048576 | tf_op jit(solution)/shard_map/all_to_all | solution.py:12
  242.7 15.8 %all-to-all-start.5 = ((f32[8,16,4,128]{3,2,1,0:T(4,128)}), f32[8,16,4,128]{3,2,1,0:T(4,128)S(1)}, u32[]{:S(2)}, u32[]{:S(2)}) async-start(f32[8,16,4,128]{3,2,1,0:T(4,128)} %bitcast.84), calls=%async_computation.5 | async-start | bytes 524288 | tf_op jit(solution)/shard_map/all_to_all | solution.py:35
where the time goes:
time: 263 us; the launch traced here: 259 us
  blocking collectives  104 us (40%)
  waiting for transfers between devices  89.5 us (34%)
  starting transfers between devices  32.7 us (12%)
  between operations  13.1 us (5%)
  matrix products  10.5 us (4%)
  local copies, waits for them, and re-layouts  8.26 us (3%)
    psum x15, blocking collectives, spread(): array = lax.psum(array, axis)  104 us
    all_to_all x5, waiting for transfers between devices, sent_to_all(): lax.all_to_all(jnp.broadcast_to(array[None], (peers, *array.shape)), axis...  78.6 us
    all_to_all x5, starting transfers between devices, sent_to_all(): lax.all_to_all(jnp.broadcast_to(array[None], (peers, *array.shape)), axis...  28 us
    all_to_all x1, waiting for transfers between devices, summed_on_arrival(): lax.all_to_all(pieces, axis, split_axis=0, concat_axis=0, tiled=True)  10.9 us
    dot_general x5, matrix products, per_device(): lax.dot_general(sent_block, panel_rows, (((1,), (1,)), ((), ())), preferr...  7.98 us
  transfers between devices with their start and end apart: 6, of which 6 were waited for; matrix products, arithmetic and copies ran while one was open for 0% of the time, Pallas kernels for 0%

commit v1 on v0

v1 whole, which is shorter than its diff:
```python
import functools
import itertools

import jax
import jax.numpy as jnp
from jax import lax
from jax.experimental import pallas as pl
from jax.experimental.pallas import tpu as pltpu
from jax.sharding import Mesh
from jax.sharding import PartitionSpec as P

MESH = pl.DeviceIdType.MESH
COL = ("y", "x", "core")
LANES = 128


def first_of(t):
    return t * (t - 1) // 2


def kernel(
    sizes,
    sections,
    order,
    live,
    f_hbm,
    d_hbm,
    rhs,
    out,
    fac,
    inv,
    low,
    core_out,
    core_in,
    plane_out,
    plane_in,
    chunk,
    b_out,
    b_in,
    z_out,
    z_in,
    x_all,
    total,
    f_out,
    f_in,
    local_sem,
    send_sem,
    recv_sem,
):
    nz, ny, nx = sizes
    chips = ny * nx
    tile = nz * LANES
    half = tile // 2
    rows_dev = rhs.shape[1]
    z = lax.axis_index("row")
    y = lax.axis_index("y")
    x = lax.axis_index("x")
    core = lax.axis_index("core")
    chip = y * nx + x
    col = chip * 2 + core

    phase_of = {}

    def phase(*key):
        return phase_of.setdefault(key, len(phase_of))

    pending = []

    def send(key, src, dst, device):
        number = phase(*key)
        pltpu.make_async_remote_copy(
            src_ref=src,
            dst_ref=dst,
            send_sem=send_sem.at[number],
            recv_sem=recv_sem.at[number],
            device_id=device,
            device_id_type=MESH,
        ).start()

    def arrived(key, like):
        pltpu.make_async_copy(like, like, recv_sem.at[phase(*key)]).wait()

    steps = sorted(
        [o for o in itertools.product(range(ny), range(nx)) if any(o)],
        key=lambda o: -(min(o[0], ny - o[0]) + min(o[1], nx - o[1])),
    )

    def chip_at(step):
        return lax.rem(y + step[0], ny), lax.rem(x + step[1], nx)

    def z_at(step):
        return lax.rem(z + step, nz)

    z_steps = sorted(range(1, nz), key=lambda o: -min(o, nz - o))

    fac_copies = []
    for u in range(sections):
        copy = pltpu.make_async_copy(f_hbm.at[u], fac.at[u], local_sem.at[u])
        copy.start()
        fac_copies.append(copy)
    inv_copy = pltpu.make_async_copy(d_hbm, inv, local_sem.at[sections])
    inv_copy.start()

    barrier = pltpu.get_barrier_semaphore()
    count = 0
    for step in steps:
        py, px = chip_at(step)
        for other in range(2):
            pl.semaphore_signal(
                barrier,
                inc=1,
                device_id={"y": py, "x": px, "core": (core + other) % 2},
                device_id_type=MESH,
            )
            count += 1
    pl.semaphore_signal(barrier, inc=1, device_id={"core": 1 - core}, device_id_type=MESH)
    count += 1
    for step in z_steps:
        pl.semaphore_signal(barrier, inc=1, device_id={"row": z_at(step)}, device_id_type=MESH)
        count += 1

    slots = [jnp.full((chips, LANES), order[t], jnp.int32) for t in range(sections)]
    own_slot = [[slots[t] == col * rows_dev + l for l in range(rows_dev)] for t in range(sections)]

    b_out[...] = jnp.zeros_like(b_out)
    for t in range(sections):
        value = jnp.zeros((chips, LANES), jnp.float32)
        for l in range(rows_dev):
            value = jnp.where(own_slot[t][l], rhs[:, l, :], value)
        b_out[:, t, :] = value

    masks = [
        [
            jnp.where(own_slot[t][l], 1.0, 0.0).astype(jnp.bfloat16)[None]
            for l in range(rows_dev)
        ]
        for t in range(sections)
    ]

    def own_half(t, u, part):
        value = None
        for l in range(rows_dev):
            start = pl.multiple_of(l * tile + part * half, half)
            rows = fac[u, pl.ds(start, half), :].reshape(half // chips, chips, LANES)
            rows = rows * masks[t][l]
            value = rows if value is None else value + rows
        return value.reshape(chips, half // chips, LANES)

    for u in range(sections):
        fac_copies[u].wait()
    for t in range(1, sections):
        for u in range(t):
            core_out[first_of(t) + u] = own_half(t, u, 1 - core)
            plane_out[first_of(t) + u] = own_half(t, u, core)

    pl.semaphore_wait(barrier, count)

    for step in steps:
        py, px = chip_at(step)
        for other in range(2):
            send(
                ("b",),
                b_out.at[py * nx + px],
                b_in.at[col],
                {"y": py, "x": px, "core": (core + other) % 2},
            )
    send(("b",), b_out.at[chip], b_in.at[col], {"core": 1 - core})
    b_in[col] = b_out[chip]

    def tiles_of(t):
        return pl.ds(first_of(t), t)

    for t in range(1, sections):
        send(("core", t), core_out.at[tiles_of(t)], core_in.at[tiles_of(t)], {"core": 1 - core})

    def scatter(t):
        arrived(("core", t), core_in.at[tiles_of(t)])
        for u in range(t):
            q = first_of(t) + u
            plane_out[q] = plane_out[q] + core_in[q]
            plane_in[chip, q] = plane_out[q, chip]
        for step in steps:
            py, px = chip_at(step)
            send(
                ("scatter", t),
                plane_out.at[tiles_of(t), py * nx + px],
                plane_in.at[chip, tiles_of(t)],
                {"y": py, "x": px},
            )

    def gather(t):
        arrived(("scatter", t), plane_in.at[pl.ds(0, chips - 1), tiles_of(t)])
        for u in range(t):
            q = first_of(t) + u
            value = plane_in[0, q]
            for j in range(1, chips):
                value = value + plane_in[j, q]
            chunk[q] = value
            low[q, core, chip] = value
        for step in steps:
            py, px = chip_at(step)
            send(
                ("gather", t),
                chunk.at[tiles_of(t)],
                low.at[tiles_of(t), core, chip],
                {"y": py, "x": px},
            )

    def swap(t):
        arrived(("gather", t), low.at[tiles_of(t), 0, pl.ds(0, chips - 1)])
        send(
            ("swap", t),
            low.at[tiles_of(t), core],
            low.at[tiles_of(t), core],
            {"core": 1 - core},
        )

    def swapped(t):
        arrived(("swap", t), low.at[tiles_of(t), 0])

    block_row = lax.broadcasted_iota(jnp.int32, (nz, LANES), 0)
    held = [jnp.zeros((nz, LANES), jnp.float32) for _ in range(sections)]
    sent = [None] * sections

    def product(t, u):
        weights = low[first_of(t) + u].reshape(tile, LANES)
        full = lax.dot_general(
            sent[u], weights, (((1,), (1,)), ((), ())), preferred_element_type=jnp.float32
        )
        value = jnp.zeros((nz, LANES), jnp.float32)
        for k in range(nz):
            value = jnp.where(block_row == k, full[0:nz, k * LANES : (k + 1) * LANES], value)
        return value

    def ask(t, b_all):
        value = jnp.where(block_row == z, b_all[t : t + 1, :], 0.0) - held[t]
        z_out[t] = value
        z_in[t, z] = value
        for step in z_steps:
            send(("z", t), z_out.at[t], z_in.at[t, z], {"row": z_at(step)})

    def solve(t):
        arrived(("z", t), z_in.at[t, pl.ds(0, nz - 1)])
        remaining = z_in[t, 0]
        for k in range(1, nz):
            remaining = remaining + z_in[t, k]
        high = remaining.astype(jnp.bfloat16).astype(jnp.float32)
        rest = remaining - high
        mid = rest.astype(jnp.bfloat16).astype(jnp.float32)
        pieces = jnp.concatenate([high, mid, rest - mid, jnp.zeros_like(high)], axis=0)
        piece_row = lax.broadcasted_iota(jnp.int32, (4 * nz, LANES), 0) % nz
        spread = jnp.concatenate(
            [jnp.where(piece_row == k, pieces, 0.0) for k in range(nz)], axis=1
        ).astype(jnp.bfloat16)
        parts = lax.dot_general(
            spread, inv[t], (((1,), (1,)), ((), ())), preferred_element_type=jnp.float32
        )
        solved = jnp.sum(parts, axis=0, keepdims=True)
        x_all[t, chip] = solved
        for step in steps:
            py, px = chip_at(step)
            send(("x", t), x_all.at[t, chip], x_all.at[t, chip], {"y": py, "x": px})
        kept = jnp.where(t < my_live, jnp.broadcast_to(solved, (chips, LANES)), 0.0)
        sent[t] = kept.astype(jnp.bfloat16)

    rhs_row = lax.broadcasted_iota(jnp.int32, (chips, LANES), 0)
    live_rows = jnp.zeros((chips, LANES), jnp.int32)
    for j in range(chips):
        live_rows = jnp.where(rhs_row == j, live[j], live_rows)
    my_live = jnp.full((chips, LANES), live[chip], jnp.int32)
    solved_all = [None] * sections

    def update(u):
        arrived(("x", u), x_all.at[u, pl.ds(0, chips - 1)])
        rows = jnp.concatenate([x_all[u, j] for j in range(chips)], axis=0)
        solved_all[u] = rows
        block = jnp.where(u < live_rows, rows, 0.0).astype(jnp.bfloat16)
        for l in range(rows_dev):
            part = lax.dot_general(
                block,
                fac[u, l * tile : (l + 1) * tile, :],
                (((1,), (1,)), ((), ())),
                preferred_element_type=jnp.float32,
            )
            total[l] = part if u == 0 else total[l] + part

    scatter(1)
    scatter(2)
    arrived(("b",), b_in.at[pl.ds(0, 2 * chips - 1)])
    b_all = b_in[0]
    for j in range(1, 2 * chips):
        b_all = b_all + b_in[j]
    ask(0, b_all)
    gather(1)
    scatter(3)
    gather(2)
    scatter(4)
    inv_copy.wait()
    solve(0)
    swap(1)
    swapped(1)
    held[1] = held[1] + product(1, 0)
    ask(1, b_all)
    swap(2)
    gather(3)
    swapped(2)
    held[2] = held[2] + product(2, 0)
    solve(1)
    held[2] = held[2] + product(2, 1)
    ask(2, b_all)
    swap(3)
    gather(4)
    update(0)
    swapped(3)
    held[3] = held[3] + product(3, 0) + product(3, 1)
    solve(2)
    held[3] = held[3] + product(3, 2)
    ask(3, b_all)
    update(1)
    swap(4)
    swapped(4)
    held[4] = held[4] + product(4, 0) + product(4, 1) + product(4, 2)
    solve(3)
    held[4] = held[4] + product(4, 3)
    ask(4, b_all)
    update(2)
    update(3)
    solve(4)
    update(4)

    for k in range(nz):
        f_out[k] = total[:, :, k * LANES : (k + 1) * LANES].astype(jnp.bfloat16)
    for step in z_steps:
        to = z_at(step)
        send(("final",), f_out.at[to], f_in.at[z], {"row": to})
    f_in[z] = f_out[z]
    arrived(("final",), f_in.at[pl.ds(0, nz - 1)])
    for l in range(rows_dev):
        value = rhs[:, l, :]
        taken = f_in[0, l].astype(jnp.float32)
        for k in range(1, nz):
            taken = taken + f_in[k, l].astype(jnp.float32)
        value = value - taken
        for u in range(sections):
            here = (u < live_rows) & own_slot[u][l]
            value = jnp.where(here, solved_all[u], value)
        out[:, l, :] = value

    def left(key, like):
        pltpu.make_async_copy(like, like, send_sem.at[phase(*key)]).wait()

    left(("b",), b_in.at[pl.ds(0, 2 * chips - 1)])
    for t in range(1, sections):
        left(("core", t), core_out.at[tiles_of(t)])
        left(("scatter", t), plane_in.at[pl.ds(0, chips - 1), tiles_of(t)])
        left(("gather", t), plane_in.at[pl.ds(0, chips - 1), tiles_of(t)])
        left(("swap", t), low.at[tiles_of(t), 0])
    for t in range(sections):
        left(("z", t), z_in.at[t, pl.ds(0, nz - 1)])
        left(("x", t), x_all.at[t, pl.ds(0, chips - 1)])
    left(("final",), f_in.at[pl.ds(0, nz - 1)])


def per_device(sizes, factor, diag_inverse, right_side, tile_order, live_segments):
    nz, ny, nx = sizes
    sections, _, tile = diag_inverse.shape
    rhs_count, rows_dev, width = right_side.shape
    chips = ny * nx
    tiles = first_of(sections)
    part = tile // (2 * chips)
    phases = 2 + 4 * (sections - 1) + 2 * sections
    bf16, f32 = jnp.bfloat16, jnp.float32
    vmem = pltpu.VMEM
    return pl.pallas_call(
        functools.partial(kernel, sizes, sections),
        out_shape=jax.ShapeDtypeStruct(right_side.shape, f32),
        in_specs=[
            pl.BlockSpec(memory_space=pltpu.SMEM),
            pl.BlockSpec(memory_space=pltpu.SMEM),
            pl.BlockSpec(memory_space=pl.ANY),
            pl.BlockSpec(memory_space=pl.ANY),
            pl.BlockSpec(memory_space=vmem),
        ],
        out_specs=pl.BlockSpec(memory_space=vmem),
        scratch_shapes=[
            vmem((sections, rows_dev * tile, width), bf16),
            vmem((sections, width, tile), bf16),
            vmem((tiles, 2, chips, part, width), bf16),
            vmem((tiles, chips, part, width), bf16),
            vmem((tiles, chips, part, width), bf16),
            vmem((tiles, chips, part, width), bf16),
            vmem((chips, tiles, part, width), bf16),
            vmem((tiles, part, width), bf16),
            vmem((rhs_count, 8, width), f32),
            vmem((2 * chips, 8, width), f32),
            vmem((sections, nz, width), f32),
            vmem((sections, nz, nz, width), f32),
            vmem((sections, chips, 1, width), f32),
            vmem((rows_dev, rhs_count, tile), f32),
            vmem((nz, rows_dev, rhs_count, width), bf16),
            vmem((nz, rows_dev, rhs_count, width), bf16),
            pltpu.SemaphoreType.DMA((sections + 1,)),
            pltpu.SemaphoreType.DMA((phases,)),
            pltpu.SemaphoreType.DMA((phases,)),
        ],
        compiler_params=pltpu.CompilerParams(collective_id=0, has_side_effects=True),
    )(tile_order, live_segments, jnp.transpose(factor, (1, 0, 2)), diag_inverse, right_side)


def solution(mesh):
    sizes = (mesh.shape["row"], 4, 4)
    finer = Mesh(mesh.devices.reshape(mesh.shape["row"], 4, 4, 2), ("row", *COL))
    return jax.shard_map(
        functools.partial(per_device, sizes),
        mesh=finer,
        in_specs=(P(COL, None, "row"), P(None, "row", None), P(None, COL, "row"), P(), P()),
        out_specs=P(None, COL, "row"),
        check_vma=False,
    )
```

time: 263 us -> 65.1 us (0.25); the launches traced: 259 us -> 64.6 us
  blocking collectives: 104 us -> 0 us
  waiting for transfers between devices: 89.5 us -> 0 us
  Pallas kernels: 0 us -> 63.2 us
  starting transfers between devices: 32.7 us -> 0 us
  between operations: 13.1 us -> 0.01 us
  matrix products: 10.5 us -> 0 us
  local copies, waits for them, and re-layouts: 8.26 us -> 1.38 us
    psum x15 -> x0, blocking collectives: 104 us -> none  [spread(): array = lax.psum(array, axis)]
    all_to_all x6 -> x0, waiting for transfers between devices: 89.5 us -> none  [the longest x5 78.6 us: sent_to_all(): lax.all_to_all(jnp.broadcast_to(array[None], (peers, *array.shape)), axis...]
    pallas_call x0 -> x1, Pallas kernels: none -> 63.2 us  [per_device(): pl.pallas_call(functools.partial(kernel, sizes, sections), out_shape=jax....]
    all_to_all x6 -> x0, starting transfers between devices: 32.7 us -> none  [the longest x5 28 us: sent_to_all(): lax.all_to_all(jnp.broadcast_to(array[None], (peers, *array.shape)), axis...]
    dot_general x10 -> x0, matrix products: 10.5 us -> none  [the longest x5 7.98 us: per_device(): lax.dot_general(sent_block, panel_rows, (((1,), (1,)), ((), ())), preferr...]
    broadcast_in_dim x11 -> x0, local copies, waits for them, and re-layouts: 4.24 us -> none  [the longest x10 4.24 us: sent_to_all(): jnp.broadcast_to(array[None], (peers, *array.shape))]
  transfers between devices with their start and end apart: 6 -> 0, of which waited for: 6 -> 0; matrix products, arithmetic and copies ran while one was open for 0% -> 0% of each run, Pallas kernels for 0% -> 0%
where the time goes in v1:
time: 65.1 us; the launch traced here: 64.6 us
  Pallas kernels  63.2 us (97%)
  local copies, waits for them, and re-layouts  1.38 us (2%)
    pallas_call x1, Pallas kernels, per_device(): pl.pallas_call(functools.partial(kernel, sizes, sections), out_shape=jax....  63.2 us
    unnamed x1, local copies, waits for them, and re-layouts  1.38 us

profile of v1, /device:TPU:32, one launch (start us, length us, event | category | flops | bytes accessed | tf_op | source)
XLA Modules:
  0.0 64.6 jit_solution(7458237632872023059)
XLA Ops:
  0.0 63.2 %shard_map.55 = f32[16,4,128]{2,1,0:T(4,128)} custom-call(s32[128]{0:T(128)} %order.1, s32[16]{0:T(128)} %live.1, bf16[5,4096,128]{2,1,0:T(8,128)(2,1)} %bitcast.1, bf16[5,128,1024]{2,1,0:T(8,128)(2,1)} %d_hbm.1, f32[16,4,128]{2,1,0:T(4,128)} %rhs.1), custom_call_target="tpu_custom_call" | custom-call | tf_op jit(solution)/shard_map/pallas_call | solution.py:374
  63.2 1.4 %copy.7 = f32[16,4,128]{2,1,0:T(4,128)} copy(f32[16,4,128]{2,1,0:T(4,128)} %shard_map.55) | data formatting | bytes 65536

commit v2 on v1

--- a/solution.py
+++ b/solution.py
@@ -14,8 +14,19 @@
 LANES = 128
 
 
+NEAR = 2
+
+
+def moved(t):
+    return range(max(0, t - NEAR), t)
+
+
 def first_of(t):
-    return t * (t - 1) // 2
+    return sum(len(moved(s)) for s in range(1, t))
+
+
+def place_of(t, u):
+    return first_of(t) + u - moved(t)[0]
 
 
 def kernel(
@@ -41,6 +52,8 @@
     z_in,
     x_all,
     total,
+    back_out,
+    back_in,
     f_out,
     f_in,
     local_sem,
@@ -93,14 +106,6 @@
 
     z_steps = sorted(range(1, nz), key=lambda o: -min(o, nz - o))
 
-    fac_copies = []
-    for u in range(sections):
-        copy = pltpu.make_async_copy(f_hbm.at[u], fac.at[u], local_sem.at[u])
-        copy.start()
-        fac_copies.append(copy)
-    inv_copy = pltpu.make_async_copy(d_hbm, inv, local_sem.at[sections])
-    inv_copy.start()
-
     barrier = pltpu.get_barrier_semaphore()
     count = 0
     for step in steps:
@@ -113,21 +118,29 @@
                 device_id_type=MESH,
             )
             count += 1
-    pl.semaphore_signal(barrier, inc=1, device_id={"core": 1 - core}, device_id_type=MESH)
-    count += 1
     for step in z_steps:
         pl.semaphore_signal(barrier, inc=1, device_id={"row": z_at(step)}, device_id_type=MESH)
         count += 1
+    pl.semaphore_signal(barrier, inc=1, device_id={"core": 1 - core}, device_id_type=MESH)
+    count += 1
+
+    fac_copies = []
+    for u in range(sections):
+        copy = pltpu.make_async_copy(f_hbm.at[u], fac.at[u], local_sem.at[u])
+        copy.start()
+        fac_copies.append(copy)
+    inv_copy = pltpu.make_async_copy(d_hbm, inv, local_sem.at[sections])
+    inv_copy.start()
 
     slots = [jnp.full((chips, LANES), order[t], jnp.int32) for t in range(sections)]
     own_slot = [[slots[t] == col * rows_dev + l for l in range(rows_dev)] for t in range(sections)]
 
-    b_out[...] = jnp.zeros_like(b_out)
     for t in range(sections):
         value = jnp.zeros((chips, LANES), jnp.float32)
         for l in range(rows_dev):
             value = jnp.where(own_slot[t][l], rhs[:, l, :], value)
-        b_out[:, t, :] = value
+        for j in range(chips):
+            b_out[j, t] = value[j : j + 1]
 
     masks = [
         [
@@ -146,37 +159,45 @@
             value = rows if value is None else value + rows
         return value.reshape(chips, half // chips, LANES)
 
-    for u in range(sections):
-        fac_copies[u].wait()
-    for t in range(1, sections):
-        for u in range(t):
-            core_out[first_of(t) + u] = own_half(t, u, 1 - core)
-            plane_out[first_of(t) + u] = own_half(t, u, core)
-
-    pl.semaphore_wait(barrier, count)
-
-    for step in steps:
-        py, px = chip_at(step)
-        for other in range(2):
-            send(
-                ("b",),
-                b_out.at[py * nx + px],
-                b_in.at[col],
-                {"y": py, "x": px, "core": (core + other) % 2},
-            )
-    send(("b",), b_out.at[chip], b_in.at[col], {"core": 1 - core})
+    def tiles_of(t):
+        return pl.ds(first_of(t), len(moved(t)))
+
+    def share(t):
+        for u in moved(t):
+            core_out[place_of(t, u)] = own_half(t, u, 1 - core)
+        send(("core", t), core_out.at[tiles_of(t)], core_in.at[tiles_of(t)], {"core": 1 - core})
+
+    def keep_own(t):
+        for u in moved(t):
+            plane_out[place_of(t, u)] = own_half(t, u, core)
+
+    def to_chips(key, source, target):
+        for step in steps:
+            py, px = chip_at(step)
+            for other in range(2):
+                send(
+                    key,
+                    source.at[py * nx + px],
+                    target.at[col],
+                    {"y": py, "x": px, "core": (core + other) % 2},
+                )
+        send(key, source.at[chip], target.at[col], {"core": 1 - core})
+
+    def from_chips(key, target):
+        arrived(key, target.at[pl.ds(0, 2 * chips - 1)])
+        value = target[0]
+        for j in range(1, 2 * chips):
+            value = value + target[j]
+        return value
+
+    with jax.named_scope("barrier"):
+        pl.semaphore_wait(barrier, count)
+    to_chips(("b",), b_out, b_in)
     b_in[col] = b_out[chip]
-
-    def tiles_of(t):
-        return pl.ds(first_of(t), t)
-
-    for t in range(1, sections):
-        send(("core", t), core_out.at[tiles_of(t)], core_in.at[tiles_of(t)], {"core": 1 - core})
 
     def scatter(t):
         arrived(("core", t), core_in.at[tiles_of(t)])
-        for u in range(t):
-            q = first_of(t) + u
+        for q in range(first_of(t), first_of(t + 1)):
             plane_out[q] = plane_out[q] + core_in[q]
             plane_in[chip, q] = plane_out[q, chip]
         for step in steps:
@@ -190,8 +211,7 @@
 
     def gather(t):
         arrived(("scatter", t), plane_in.at[pl.ds(0, chips - 1), tiles_of(t)])
-        for u in range(t):
-            q = first_of(t) + u
+        for q in range(first_of(t), first_of(t + 1)):
             value = plane_in[0, q]
             for j in range(1, chips):
                 value = value + plane_in[j, q]
@@ -223,7 +243,7 @@
     sent = [None] * sections
 
     def product(t, u):
-        weights = low[first_of(t) + u].reshape(tile, LANES)
+        weights = low[place_of(t, u)].reshape(tile, LANES)
         full = lax.dot_general(
             sent[u], weights, (((1,), (1,)), ((), ())), preferred_element_type=jnp.float32
         )
@@ -232,8 +252,11 @@
             value = jnp.where(block_row == k, full[0:nz, k * LANES : (k + 1) * LANES], value)
         return value
 
+    def add(t, u):
+        held[t] = held[t] + product(t, u)
+
     def ask(t, b_all):
-        value = jnp.where(block_row == z, b_all[t : t + 1, :], 0.0) - held[t]
+        value = jnp.where(block_row == z, b_all[t], 0.0) - held[t]
         z_out[t] = value
         z_in[t, z] = value
         for step in z_steps:
@@ -284,47 +307,76 @@
             )
             total[l] = part if u == 0 else total[l] + part
 
+    def back(t):
+        i = t - NEAR - 1
+        for k in range(nz):
+            value = jnp.zeros((chips, LANES), jnp.float32)
+            for l in range(rows_dev):
+                part = total[l, :, k * LANES : (k + 1) * LANES]
+                value = jnp.where(own_slot[t][l], part, value)
+            back_out[i, :, k, :] = value
+        to_chips(("back", t), back_out.at[i], back_in.at[i])
+        back_in[i, col] = back_out[i, chip]
+
+    def backed(t):
+        i = t - NEAR - 1
+        held[t] = held[t] + from_chips(("back", t), back_in.at[i])
+
+    fac_copies[0].wait()
+    share(1)
+    keep_own(1)
+    fac_copies[1].wait()
+    share(2)
     scatter(1)
+    keep_own(2)
     scatter(2)
-    arrived(("b",), b_in.at[pl.ds(0, 2 * chips - 1)])
-    b_all = b_in[0]
-    for j in range(1, 2 * chips):
-        b_all = b_all + b_in[j]
+    fac_copies[2].wait()
+    share(3)
+    fac_copies[3].wait()
+    share(4)
+    keep_own(3)
+    keep_own(4)
+    b_all = from_chips(("b",), b_in)
     ask(0, b_all)
     gather(1)
     scatter(3)
     gather(2)
-    scatter(4)
     inv_copy.wait()
     solve(0)
+    scatter(4)
     swap(1)
     swapped(1)
-    held[1] = held[1] + product(1, 0)
+    add(1, 0)
     ask(1, b_all)
+    gather(3)
     swap(2)
-    gather(3)
+    update(0)
+    back(3)
     swapped(2)
-    held[2] = held[2] + product(2, 0)
+    add(2, 0)
     solve(1)
-    held[2] = held[2] + product(2, 1)
+    add(2, 1)
     ask(2, b_all)
+    gather(4)
     swap(3)
-    gather(4)
-    update(0)
+    update(1)
+    back(4)
     swapped(3)
-    held[3] = held[3] + product(3, 0) + product(3, 1)
+    add(3, 1)
+    backed(3)
     solve(2)
-    held[3] = held[3] + product(3, 2)
+    add(3, 2)
     ask(3, b_all)
-    update(1)
     swap(4)
     swapped(4)
-    held[4] = held[4] + product(4, 0) + product(4, 1) + product(4, 2)
+    add(4, 2)
+    backed(4)
+    update(2)
     solve(3)
-    held[4] = held[4] + product(4, 3)
+    add(4, 3)
     ask(4, b_all)
-    update(2)
     update(3)
+    fac_copies[4].wait()
     solve(4)
     update(4)
 
@@ -334,17 +386,15 @@
         to = z_at(step)
         send(("final",), f_out.at[to], f_in.at[z], {"row": to})
     f_in[z] = f_out[z]
-    arrived(("final",), f_in.at[pl.ds(0, nz - 1)])
+    bases = []
     for l in range(rows_dev):
-        value = rhs[:, l, :]
-        taken = f_in[0, l].astype(jnp.float32)
-        for k in range(1, nz):
-            taken = taken + f_in[k, l].astype(jnp.float32)
-        value = value - taken
+        base = rhs[:, l, :]
+        scale = jnp.ones_like(base)
         for u in range(sections):
             here = (u < live_rows) & own_slot[u][l]
-            value = jnp.where(here, solved_all[u], value)
-        out[:, l, :] = value
+            base = jnp.where(here, solved_all[u], base)
+            scale = jnp.where(here, 0.0, scale)
+        bases.append((base, scale))
 
     def left(key, like):
         pltpu.make_async_copy(like, like, send_sem.at[phase(*key)]).wait()
@@ -355,9 +405,19 @@
         left(("scatter", t), plane_in.at[pl.ds(0, chips - 1), tiles_of(t)])
         left(("gather", t), plane_in.at[pl.ds(0, chips - 1), tiles_of(t)])
         left(("swap", t), low.at[tiles_of(t), 0])
+    for t in range(NEAR + 1, sections):
+        left(("back", t), back_in.at[t - NEAR - 1, pl.ds(0, 2 * chips - 1)])
     for t in range(sections):
         left(("z", t), z_in.at[t, pl.ds(0, nz - 1)])
         left(("x", t), x_all.at[t, pl.ds(0, chips - 1)])
+
+    arrived(("final",), f_in.at[pl.ds(0, nz - 1)])
+    for l in range(rows_dev):
+        taken = f_in[0, l].astype(jnp.float32)
+        for k in range(1, nz):
+            taken = taken + f_in[k, l].astype(jnp.float32)
+        base, scale = bases[l]
+        out[:, l, :] = base - jnp.where(scale > 0.5, taken, 0.0)
     left(("final",), f_in.at[pl.ds(0, nz - 1)])
 
 
@@ -368,7 +428,7 @@
     chips = ny * nx
     tiles = first_of(sections)
     part = tile // (2 * chips)
-    phases = 2 + 4 * (sections - 1) + 2 * sections
+    phases = 2 + 4 * (sections - 1) + 2 * sections + sections - NEAR - 1
     bf16, f32 = jnp.bfloat16, jnp.float32
     vmem = pltpu.VMEM
     return pl.pallas_call(
@@ -391,12 +451,14 @@
             vmem((tiles, chips, part, width), bf16),
             vmem((chips, tiles, part, width), bf16),
             vmem((tiles, part, width), bf16),
-            vmem((rhs_count, 8, width), f32),
-            vmem((2 * chips, 8, width), f32),
+            vmem((rhs_count, sections, 1, width), f32),
+            vmem((2 * chips, sections, 1, width), f32),
             vmem((sections, nz, width), f32),
             vmem((sections, nz, nz, width), f32),
             vmem((sections, chips, 1, width), f32),
             vmem((rows_dev, rhs_count, tile), f32),
+            vmem((sections - NEAR - 1, chips, nz, width), f32),
+            vmem((sections - NEAR - 1, 2 * chips, nz, width), f32),
             vmem((nz, rows_dev, rhs_count, width), bf16),
             vmem((nz, rows_dev, rhs_count, width), bf16),
             pltpu.SemaphoreType.DMA((sections + 1,)),

time: 65.1 us -> 58.6 us (0.900)
  Pallas kernels: 63.2 us -> 57 us
    pallas_call x1, Pallas kernels: 63.2 us -> 57 us  [per_device(): pl.pallas_call(functools.partial(kernel, sizes, sections), out_shape=jax....]
where the time goes in v2:
time: 58.6 us; the launch traced here: 58.4 us
  Pallas kernels  57 us (97%)
  local copies, waits for them, and re-layouts  1.38 us (2%)
    pallas_call x1, Pallas kernels, per_device(): pl.pallas_call(functools.partial(kernel, sizes, sections), out_shape=jax....  57 us
    unnamed x1, local copies, waits for them, and re-layouts  1.38 us

profile of v2, /device:TPU:32, one launch (start us, length us, event | category | flops | bytes accessed | tf_op | source)
XLA Modules:
  0.0 58.4 jit_solution(17936390588573339493)
XLA Ops:
  0.0 57.0 %shard_map.55 = f32[16,4,128]{2,1,0:T(4,128)} custom-call(s32[128]{0:T(128)} %order.1, s32[16]{0:T(128)} %live.1, bf16[5,4096,128]{2,1,0:T(8,128)(2,1)} %bitcast.1, bf16[5,128,1024]{2,1,0:T(8,128)(2,1)} %d_hbm.1, f32[16,4,128]{2,1,0:T(4,128)} %rhs.1), custom_call_target="tpu_custom_call" | custom-call | tf_op jit(solution)/shard_map/pallas_call | solution.py:434
  57.0 1.4 %copy.7 = f32[16,4,128]{2,1,0:T(4,128)} copy(f32[16,4,128]{2,1,0:T(4,128)} %shard_map.55) | data formatting | bytes 65536

commit v3 on v2

--- a/solution.py
+++ b/solution.py
@@ -32,12 +32,15 @@
 def kernel(
     sizes,
     sections,
+    order_hbm,
+    live_hbm,
+    f_hbm,
+    d_hbm,
+    rhs_hbm,
+    out,
     order,
     live,
-    f_hbm,
-    d_hbm,
     rhs,
-    out,
     fac,
     inv,
     low,
@@ -124,6 +127,11 @@
     pl.semaphore_signal(barrier, inc=1, device_id={"core": 1 - core}, device_id_type=MESH)
     count += 1
 
+    small_copies = []
+    for i, (src, dst) in enumerate([(order_hbm, order), (rhs_hbm, rhs), (live_hbm, live)]):
+        copy = pltpu.make_async_copy(src, dst, local_sem.at[sections + 1 + i])
+        copy.start()
+        small_copies.append(copy)
     fac_copies = []
     for u in range(sections):
         copy = pltpu.make_async_copy(f_hbm.at[u], fac.at[u], local_sem.at[u])
@@ -131,6 +139,8 @@
         fac_copies.append(copy)
     inv_copy = pltpu.make_async_copy(d_hbm, inv, local_sem.at[sections])
     inv_copy.start()
+    for copy in small_copies:
+        copy.wait()
 
     slots = [jnp.full((chips, LANES), order[t], jnp.int32) for t in range(sections)]
     own_slot = [[slots[t] == col * rows_dev + l for l in range(rows_dev)] for t in range(sections)]
@@ -185,9 +195,9 @@
 
     def from_chips(key, target):
         arrived(key, target.at[pl.ds(0, 2 * chips - 1)])
-        value = target[0]
+        value = target[0].astype(jnp.float32)
         for j in range(1, 2 * chips):
-            value = value + target[j]
+            value = value + target[j].astype(jnp.float32)
         return value
 
     with jax.named_scope("barrier"):
@@ -314,7 +324,7 @@
             for l in range(rows_dev):
                 part = total[l, :, k * LANES : (k + 1) * LANES]
                 value = jnp.where(own_slot[t][l], part, value)
-            back_out[i, :, k, :] = value
+            back_out[i, :, k, :] = value.astype(back_out.dtype)
         to_chips(("back", t), back_out.at[i], back_in.at[i])
         back_in[i, col] = back_out[i, chip]
 
@@ -340,18 +350,18 @@
     ask(0, b_all)
     gather(1)
     scatter(3)
-    gather(2)
     inv_copy.wait()
     solve(0)
+    gather(2)
     scatter(4)
     swap(1)
     swapped(1)
     add(1, 0)
     ask(1, b_all)
     gather(3)
-    swap(2)
     update(0)
     back(3)
+    swap(2)
     swapped(2)
     add(2, 0)
     solve(1)
@@ -359,25 +369,25 @@
     ask(2, b_all)
     gather(4)
     swap(3)
-    update(1)
-    back(4)
     swapped(3)
     add(3, 1)
     backed(3)
     solve(2)
     add(3, 2)
     ask(3, b_all)
+    update(1)
+    back(4)
     swap(4)
     swapped(4)
     add(4, 2)
     backed(4)
-    update(2)
     solve(3)
     add(4, 3)
     ask(4, b_all)
-    update(3)
+    update(2)
     fac_copies[4].wait()
     solve(4)
+    update(3)
     update(4)
 
     for k in range(nz):
@@ -433,16 +443,19 @@
     vmem = pltpu.VMEM
     return pl.pallas_call(
         functools.partial(kernel, sizes, sections),
-        out_shape=jax.ShapeDtypeStruct(right_side.shape, f32),
+        out_shape=vmem(right_side.shape, f32),
         in_specs=[
-            pl.BlockSpec(memory_space=pltpu.SMEM),
-            pl.BlockSpec(memory_space=pltpu.SMEM),
             pl.BlockSpec(memory_space=pl.ANY),
             pl.BlockSpec(memory_space=pl.ANY),
-            pl.BlockSpec(memory_space=vmem),
+            pl.BlockSpec(memory_space=pl.ANY),
+            pl.BlockSpec(memory_space=pl.ANY),
+            pl.BlockSpec(memory_space=pl.ANY),
         ],
         out_specs=pl.BlockSpec(memory_space=vmem),
         scratch_shapes=[
+            pltpu.SMEM(tile_order.shape, jnp.int32),
+            pltpu.SMEM(live_segments.shape, jnp.int32),
+            vmem(right_side.shape, f32),
             vmem((sections, rows_dev * tile, width), bf16),
             vmem((sections, width, tile), bf16),
             vmem((tiles, 2, chips, part, width), bf16),
@@ -457,11 +470,11 @@
             vmem((sections, nz, nz, width), f32),
             vmem((sections, chips, 1, width), f32),
             vmem((rows_dev, rhs_count, tile), f32),
-            vmem((sections - NEAR - 1, chips, nz, width), f32),
-            vmem((sections - NEAR - 1, 2 * chips, nz, width), f32),
+            vmem((sections - NEAR - 1, chips, nz, width), bf16),
+            vmem((sections - NEAR - 1, 2 * chips, nz, width), bf16),
             vmem((nz, rows_dev, rhs_count, width), bf16),
             vmem((nz, rows_dev, rhs_count, width), bf16),
-            pltpu.SemaphoreType.DMA((sections + 1,)),
+            pltpu.SemaphoreType.DMA((sections + 4,)),
             pltpu.SemaphoreType.DMA((phases,)),
             pltpu.SemaphoreType.DMA((phases,)),
         ],

time: 58.6 us -> 54.7 us (0.933)
  Pallas kernels: 57 us -> 54 us
  local copies, waits for them, and re-layouts: 1.38 us -> 0.62 us
    pallas_call x1, Pallas kernels: 57 us -> 54 us  [per_device(): pl.pallas_call(functools.partial(kernel, sizes, sections), out_shape=vmem...]
    unnamed x1, local copies, waits for them, and re-layouts: 1.38 us -> 0.62 us
where the time goes in v3:
time: 54.7 us; the launch traced here: 54.6 us
  Pallas kernels  54 us (99%)
  local copies, waits for them, and re-layouts  0.62 us (1%)
    pallas_call x1, Pallas kernels, per_device(): pl.pallas_call(functools.partial(kernel, sizes, sections), out_shape=vmem...  54 us

profile of v3, /device:TPU:32, one launch (start us, length us, event | category | flops | bytes accessed | tf_op | source)
XLA Modules:
  0.0 54.6 jit_solution(92355770433713925)
XLA Ops:
  0.0 54.0 %shard_map.55 = f32[16,4,128]{2,1,0:T(4,128)S(1)} custom-call(s32[128]{0:T(128)} %order_hbm.1, s32[16]{0:T(128)} %live_hbm.1, bf16[5,4096,128]{2,1,0:T(8,128)(2,1)} %bitcast.1, bf16[5,128,1024]{2,1,0:T(8,128)(2,1)} %d_hbm.1, f32[16,4,128]{2,1,0:T(4,128)} %rhs_hbm.1), custom_call_target="tpu_custom_call" | custom-call | tf_op jit(solution)/shard_map/pallas_call | solution.py:444
  54.0 0.6 %copy.7 = f32[16,4,128]{2,1,0:T(4,128)} copy(f32[16,4,128]{2,1,0:T(4,128)S(1)} %shard_map.55) | data formatting | bytes 65536
